TPU v7x, 32 devices: a whole 2x2x4 slice. The times are simulated.
32 devices in a mesh: blk: 16 (over z, y, core), row: 2 (over x).
Axes of the slice: x: 2, y: 2, z: 4, core: 2. Of those that a mesh axis runs over, the one named last changes fastest.
Arguments:
- features: float32 [2048, 256], P(('blk', 'row')), may hold values from -2 to 2, as said below
- probes: float32 [2048, 128], P(('blk', 'row')), may hold values from -6 to 6
- outputscale: float32 [1], replicated, may hold values from 0.05 to 0.2
- noise: float32 [1], replicated, may hold values from 0.5 to 2
- pivots: int32 [256], replicated, may hold values from 0 to 2047, as said below
Outputs:
- product: float32 [2048, 128], P(('blk', 'row'))
- preconditioned: float32 [2048, 128], P(('blk', 'row'))
Inputs may be any that keep to these rules, and one draw needn't show every extreme that they name: `pivots`: 256 distinct point indices. real-valued features.
All inputs are finite; a program needn't handle non-finite values.
Results may differ from a plain program's by a relative error of at most 0.0003.
Values sent between devices are 32-bit elements; how exact they have to be, the bound alone decides.
No kernel may reach another device: no remote copies, remote signals or barrier semaphores. Data moves between devices by JAX's collectives and lax.ppermute only.
A program may use at most 64 MiB of HBM per device.

v0:
```python
import jax
import jax.numpy as jnp
from jax import lax
from jax.sharding import PartitionSpec as P

STRIDE = 4
highest = lax.Precision.HIGHEST
root_five = 2.23606797749979


def shifted(block, axis, distance):
    devices = range(lax.axis_size(axis))
    route = [((i - distance) % len(devices), i) for i in devices]
    return lax.ppermute(block, axis, route)


def kernel_tile(row_feats, row_norms, col_feats, col_norms):
    inner = lax.dot_general(
        row_feats,
        col_feats,
        (((1,), (1,)), ((), ())),
        precision=highest,
        preferred_element_type=jnp.float32,
    )
    squared = jnp.maximum(row_norms[:, None] + col_norms[None, :] - 2.0 * inner, 0.0)
    scaled = root_five * jnp.sqrt(squared)
    return (1.0 + scaled + scaled * scaled / 3.0) * jnp.exp(-scaled)


def transposed_product(kernel_block, row_probes):
    return lax.dot_general(
        kernel_block,
        row_probes,
        (((0,), (0,)), ((), ())),
        precision=highest,
        preferred_element_type=jnp.float32,
    )


def quorum_members(block_count, spacing):
    half_count = block_count // 2
    members = list(range(spacing))
    reached = 0
    while reached < half_count:
        reached = reached + spacing
        members.append(reached % block_count)
    return members


def quorum_pairs(block_count, members):
    pair_list = []
    for offset in range(block_count // 2 + 1):
        chosen = None
        for lower_slot, lower_member in enumerate(members):
            for upper_slot, upper_member in enumerate(members):
                if chosen is None and (upper_member - lower_member) % block_count == offset:
                    chosen = (lower_slot, upper_slot)
        two_sided = offset != 0 and 2 * offset != block_count
        pair_list.append((chosen[0], chosen[1], two_sided))
    return pair_list


def member_sweep(fetched, fetched_norms, upper, lower_group, block_rows):
    local_rows, probe_count = fetched[upper][1].shape
    column_sums = jnp.zeros((block_rows, probe_count), jnp.float32)
    arrived_feats = lax.all_gather(fetched[upper][0], "row", axis=0, tiled=True)
    arrived_probes = lax.all_gather(fetched[upper][1], "row", axis=0, tiled=True)
    arrived_norms = jnp.sum(arrived_feats * arrived_feats, axis=1)
    updated = []
    for position, (lower, two_sided) in enumerate(lower_group):
        kernel_block = kernel_tile(
            fetched[lower][0], fetched_norms[lower], arrived_feats, arrived_norms
        )
        updated.append(
            jnp.dot(
                kernel_block, arrived_probes, precision=highest, preferred_element_type=jnp.float32
            )
        )
        if two_sided:
            current = column_sums
            column_sums = current + transposed_product(kernel_block, fetched[lower][1])
    return (tuple(updated), column_sums)


def per_device(features, probes, outputscale, noise, pivots):
    local_rows, probe_count = probes.shape
    block_count = lax.axis_size("blk")
    piece_count = lax.axis_size("row")
    piece_index = lax.axis_index("row")
    amplitude = outputscale[0]
    nugget = noise[0]
    members = quorum_members(block_count, STRIDE)
    pair_list = quorum_pairs(block_count, members)
    slot_count = len(members)
    block_rows = local_rows * piece_count
    own_norms = jnp.sum(features * features, axis=1)
    forward = [jnp.zeros((local_rows, probe_count), jnp.float32) for member in members]
    backward = [jnp.zeros((block_rows, probe_count), jnp.float32) for member in members]
    fetched = [(features, probes)]
    for member in members[1:]:
        fetched.append(shifted((features, probes), "blk", block_count - member))
    fetched_norms = [jnp.sum(entry[0] * entry[0], axis=1) for entry in fetched]
    for upper in range(slot_count):
        lower_group = [
            (lower, two_sided) for lower, target, two_sided in pair_list if target == upper
        ]
        partials, column_sums = member_sweep(fetched, fetched_norms, upper, lower_group, block_rows)
        for position, (lower, two_sided) in enumerate(lower_group):
            forward[lower] = forward[lower] + partials[position]
        backward[upper] = column_sums
    shared = lax.psum_scatter(jnp.stack(backward), "row", scatter_dimension=1, tiled=True)
    kernel_probes = forward[0] + shared[0]
    for position in range(1, slot_count):
        outgoing = forward[position] + shared[position]
        kernel_probes = kernel_probes + shifted(outgoing, "blk", members[position])
    product = amplitude * kernel_probes + nugget * probes
    flat_index = lax.axis_index("blk") * piece_count + piece_index
    offsets = pivots - flat_index * local_rows
    inside = (offsets >= 0) & (offsets < local_rows)
    picked = jnp.where(inside[:, None], features[jnp.clip(offsets, 0, local_rows - 1)], 0.0)
    pivot_feats = lax.psum(picked, ("blk", "row"))
    pivot_norms = jnp.sum(pivot_feats * pivot_feats, axis=1)
    cross = amplitude * kernel_tile(features, own_norms, pivot_feats, pivot_norms)
    gram_part = lax.dot_general(
        cross,
        cross,
        (((0,), (0,)), ((), ())),
        precision=highest,
        preferred_element_type=jnp.float32,
    )
    projected_part = lax.dot_general(
        cross,
        product,
        (((0,), (0,)), ((), ())),
        precision=highest,
        preferred_element_type=jnp.float32,
    )
    gram_sum, projected = lax.psum((gram_part, projected_part), ("blk", "row"))
    inner_pivots = amplitude * kernel_tile(pivot_feats, pivot_norms, pivot_feats, pivot_norms)
    gram = nugget * inner_pivots + gram_sum
    factor = jnp.linalg.cholesky(gram)
    coefficients = jax.scipy.linalg.cho_solve((factor, True), projected)
    preconditioned = (
        product
        - jnp.dot(cross, coefficients, precision=highest, preferred_element_type=jnp.float32)
    ) / nugget
    return (product, preconditioned)


def solution(mesh):
    in_specs = (P(("blk", "row"), None), P(("blk", "row"), None), P(), P(), P())
    out_specs = (P(("blk", "row"), None), P(("blk", "row"), None))
    return jax.shard_map(
        per_device, mesh=mesh, in_specs=in_specs, out_specs=out_specs, check_vma=False
    )
```

profile of v0, /device:TPU:0, one launch (start us, length us, event | category | flops | bytes accessed | tf_op | source)
XLA Modules:
  0.0 363.2 jit_solution(4064739874456005614)
XLA Ops:
  8.0 5.5 %collective-permute-start = (f32[64,256]{1,0:T(8,128)}, f32[64,256]{1,0:T(8,128)S(1)}, u32[]{:S(2)}, u32[]{:S(2)}) collective-permute-start(f32[64,256]{1,0:T(8,128)} %param.5), channel_id=1, source_target_pairs={{2,0},{4,2},{6,4},{8,6},{10,8},{12,10},{14,12},{16,14},{18,16},{20... | collective-permute-start | bytes 196616 | tf_op jit(solution)/shard_map/ppermute | solution.py:14
  14.4 1.4 collective-permute-start.1
  16.5 1.8 gather_fusion
  20.2 5.1 %all_gather.36 = f32[128,256]{1,0:T(8,128)S(1)} all-gather(f32[64,256]{1,0:T(8,128)S(1)} %copy-done), channel_id=1, replica_groups=mesh['blk'=16,'row'=2] {'row'}, dimensions={0}, use_global_device_ids=true | all-gather | bytes 196608 | tf_op jit(solution)/shard_map/all_gather | solution.py:66
  25.2 4.6 %all_gather.37 = f32[128,128]{1,0:T(8,128)S(1)} all-gather(f32[64,128]{1,0:T(8,128)S(1)} %copy-done.1), channel_id=1, replica_groups=mesh['blk'=16,'row'=2] {'row'}, dimensions={0}, use_global_device_ids=true | all-gather | bytes 98304 | tf_op jit(solution)/shard_map/all_gather | solution.py:67
  32.5 4.6 %all_gather.47 = f32[128,128]{1,0:T(8,128)S(1)} all-gather(f32[64,128]{1,0:T(8,128)S(1)} %collective-permute-done.9), channel_id=1, replica_groups=mesh['blk'=16,'row'=2] {'row'}, dimensions={0}, use_global_device_ids=true | all-gather | bytes 98304 | tf_op jit(solution)/shard_map/all_gather | solution.py:67
  37.1 3.2 collective-permute-start.7
  40.3 4.6 %all_gather.39 = f32[128,128]{1,0:T(8,128)S(1)} all-gather(f32[64,128]{1,0:T(8,128)S(1)} %collective-permute-done.1), channel_id=1, replica_groups=mesh['blk'=16,'row'=2] {'row'}, dimensions={0}, use_global_device_ids=true | all-gather | bytes 98304 | tf_op jit(solution)/shard_map/all_gather | solution.py:67
  44.9 1.4 collective-permute-start.3
  46.3 4.6 %all_gather.43 = f32[128,128]{1,0:T(8,128)S(1)} all-gather(f32[64,128]{1,0:T(8,128)S(1)} %collective-permute-done.5), channel_id=1, replica_groups=mesh['blk'=16,'row'=2] {'row'}, dimensions={0}, use_global_device_ids=true | all-gather | bytes 98304 | tf_op jit(solution)/shard_map/all_gather | solution.py:67
  51.0 4.6 %all_gather.45 = f32[128,128]{1,0:T(8,128)S(1)} all-gather(f32[64,128]{1,0:T(8,128)S(1)} %collective-permute-done.7), channel_id=1, replica_groups=mesh['blk'=16,'row'=2] {'row'}, dimensions={0}, use_global_device_ids=true | all-gather | bytes 98304 | tf_op jit(solution)/shard_map/all_gather | solution.py:67
  55.5 3.0 collective-permute-start.8
  58.5 4.6 %all_gather.41 = f32[128,128]{1,0:T(8,128)S(1)} all-gather(f32[64,128]{1,0:T(8,128)S(1)} %collective-permute-done.3), channel_id=1, replica_groups=mesh['blk'=16,'row'=2] {'row'}, dimensions={0}, use_global_device_ids=true | all-gather | bytes 98304 | tf_op jit(solution)/shard_map/all_gather | solution.py:67
  63.1 4.9 %all_gather.38 = f32[128,256]{1,0:T(8,128)S(1)} all-gather(f32[64,256]{1,0:T(8,128)S(1)} %collective-permute-done), channel_id=1, replica_groups=mesh['blk'=16,'row'=2] {'row'}, dimensions={0}, use_global_device_ids=true | all-gather | bytes 196608 | tf_op jit(solution)/shard_map/all_gather | solution.py:66
  68.4 5.0 %all_gather.40 = f32[128,256]{1,0:T(8,128)S(1)} all-gather(f32[64,256]{1,0:T(8,128)S(1)} %collective-permute-done.2), channel_id=1, replica_groups=mesh['blk'=16,'row'=2] {'row'}, dimensions={0}, use_global_device_ids=true | all-gather | bytes 196608 | tf_op jit(solution)/shard_map/all_gather | solution.py:66
  73.9 5.6 %all_gather.42 = f32[128,256]{1,0:T(8,128)S(1)} all-gather(f32[64,256]{1,0:T(8,128)S(1)} %collective-permute-done.4), channel_id=1, replica_groups=mesh['blk'=16,'row'=2] {'row'}, dimensions={0}, use_global_device_ids=true | all-gather | bytes 196608 | tf_op jit(solution)/shard_map/all_gather | solution.py:66
  79.9 4.9 %all_gather.46 = f32[128,256]{1,0:T(8,128)S(1)} all-gather(f32[64,256]{1,0:T(8,128)S(1)} %collective-permute-done.8), channel_id=1, replica_groups=mesh['blk'=16,'row'=2] {'row'}, dimensions={0}, use_global_device_ids=true | all-gather | bytes 196608 | tf_op jit(solution)/shard_map/all_gather | solution.py:66
  85.2 4.9 %all_gather.44 = f32[128,256]{1,0:T(8,128)S(1)} all-gather(f32[64,256]{1,0:T(8,128)S(1)} %collective-permute-done.6), channel_id=1, replica_groups=mesh['blk'=16,'row'=2] {'row'}, dimensions={0}, use_global_device_ids=true | all-gather | bytes 196608 | tf_op jit(solution)/shard_map/all_gather | solution.py:66
  95.3 52.4 %all-reduce.5.cloned.1.call-done = f32[256,256]{0,1:T(8,128)} async-done(((f32[256,256]{0,1:T(8,128)}), f32[256,256]{0,1:T(8,128)}) %all-reduce.5.cloned.1.call-update) | async-done | bytes 262160 | tf_op jit(solution)/shard_map/psum | solution.py:121
  151.2 1.5 collective-permute-start.11
  152.9 2.4 collective-permute-start.12
  155.9 2.4 collective-permute-start.14
  159.4 1.7 collective-permute-done.13
  162.4 128.9 %all-reduce.7.cloned.1.call-done = (f32[256,128]{1,0:T(8,128)}, f32[256,256]{0,1:T(8,128)}) async-done(((f32[256,128]{1,0:T(8,128)}, f32[256,256]{0,1:T(8,128)}), (f32[256,128]{1,0:T(8,128)}, f32[256,256]{0,1:T(8,128)})) %all-reduce.7.cloned.1.call-update) | async-done | bytes 393232 | tf_op jit(solution)/shard_map/psum | solution.py:138
  291.3 1.7 multiply_add_fusion
  293.2 11.7 %cholesky.49 = f32[128,128]{1,0:T(8,128)S(1)} custom-call(f32[128,128]{1,0:T(8,128)S(1)} %cholesky.115), custom_call_target="Cholesky" | custom-call | tf_op jit(solution)/shard_map/jit(cholesky)/cholesky | solution.py:141
  304.9 9.8 %custom-call.18 = f32[1,128,128]{1,2,0:T(8,128)S(1)} custom-call(f32[1,128,128]{2,1,0:T(8,128)S(1)} %get-tuple-element.29), custom_call_target="InvertDiagBlocksLowerTriangular" | custom-call | tf_op jit(solution)/shard_map/jit(cholesky)/cholesky | solution.py:141
  315.2 11.7 %cholesky.103 = f32[128,128]{1,0:T(8,128)S(1)} custom-call(f32[128,128]{1,0:T(8,128)S(1)} %convolution_subtract_fusion.2), custom_call_target="Cholesky" | custom-call | tf_op jit(solution)/shard_map/jit(cholesky)/cholesky | solution.py:141
  329.4 4.4 %while.1 = (s32[]{:T(128)}, f32[256,256]{0,1:T(8,128)S(1)}, s32[2,2]{1,0:T(2,128)S(1)}, f32[2,128,128]{2,1,0:T(8,128)S(1)}, s32[]{:T(128)}) while((s32[]{:T(128)}, f32[256,256]{0,1:T(8,128)S(1)}, s32[2,2]{1,0:T(2,128)S(1)}, f32[2,128,128]{2,1,0:T(8,128)S(1)}, s32[]{:T(128)}) %tuple.27), condition=%wide.while_cond, body=%wide.while_body.sunk | while | flops 2 | bytes 393321 | solution.py:142
  330.1 1.4 dynamic-slice.7
  332.2 1.4 dynamic-slice.7
  333.7 19.7 %custom-call.19 = f32[2,128,128]{1,2,0:T(8,128)S(1)} custom-call(f32[2,128,128]{2,1,0:T(8,128)S(1)} %get-tuple-element.9), custom_call_target="InvertDiagBlocksLowerTriangular" | custom-call | tf_op jit(solution)/shard_map/jit(_cho_solve)/triangular_solve | solution.py:142
  (123 shorter events, 23.5 us)
Async XLA Ops:
  8.0 139.7 %all-reduce.5.cloned.1.call-start = ((), (), s32[]{:S(2)}) async-start(), calls=%async_computation.2 | async-start | bytes 524288 | tf_op jit(solution)/shard_map/psum | solution.py:121
  8.0 55.0 %collective-permute-start = (f32[64,256]{1,0:T(8,128)}, f32[64,256]{1,0:T(8,128)S(1)}, u32[]{:S(2)}, u32[]{:S(2)}) collective-permute-start(f32[64,256]{1,0:T(8,128)} %param.5), channel_id=1, source_target_pairs={{2,0},{4,2},{6,4},{8,6},{10,8},{12,10},{14,12},{16,14},{18,16},{20... | collective-permute-start | bytes 196616 | tf_op jit(solution)/shard_map/ppermute | solution.py:14
  13.6 54.8 %collective-permute-start.2 = (f32[64,256]{1,0:T(8,128)}, f32[64,256]{1,0:T(8,128)S(1)}, u32[]{:S(2)}, u32[]{:S(2)}) collective-permute-start(f32[64,256]{1,0:T(8,128)} %param.5), channel_id=1, source_target_pairs={{4,0},{6,2},{8,4},{10,6},{12,8},{14,10},{16,12},{18,14},{20,16},{2... | collective-permute-start | bytes 196616 | tf_op jit(solution)/shard_map/ppermute | solution.py:14
  14.2 59.7 %collective-permute-start.4 = (f32[64,256]{1,0:T(8,128)}, f32[64,256]{1,0:T(8,128)S(1)}, u32[]{:S(2)}, u32[]{:S(2)}) collective-permute-start(f32[64,256]{1,0:T(8,128)} %param.5), channel_id=1, source_target_pairs={{6,0},{8,2},{10,4},{12,6},{14,8},{16,10},{18,12},{20,14},{22,16},{... | collective-permute-start | bytes 196616 | tf_op jit(solution)/shard_map/ppermute | solution.py:14
  14.4 22.7 %collective-permute-start.1 = (f32[64,128]{1,0:T(8,128)}, f32[64,128]{1,0:T(8,128)S(1)}, u32[]{:S(2)}, u32[]{:S(2)}) collective-permute-start(f32[64,128]{1,0:T(8,128)} %param.6), channel_id=1, source_target_pairs={{2,0},{4,2},{6,4},{8,6},{10,8},{12,10},{14,12},{16,14},{18,16},{20... | collective-permute-start | bytes 98312 | tf_op jit(solution)/shard_map/ppermute | solution.py:14
  15.8 15.9 %collective-permute-start.9 = (f32[64,128]{1,0:T(8,128)}, f32[64,128]{1,0:T(8,128)S(1)}, u32[]{:S(2)}, u32[]{:S(2)}) collective-permute-start(f32[64,128]{1,0:T(8,128)} %param.6), channel_id=1, source_target_pairs={{16,0},{18,2},{20,4},{22,6},{24,8},{26,10},{28,12},{30,14},{0,16},... | collective-permute-start | bytes 98312 | tf_op jit(solution)/shard_map/ppermute | solution.py:14
  15.8 0.7 copy-start.7
  19.2 0.8 copy-start
  19.2 129.9 %reduce-scatter.2.cloned.1.call-start = ((), (), s32[]{:S(2)}) async-start(), calls=%async_computation.1 | async-start | bytes 589824 | tf_op jit(solution)/shard_map/reduce_scatter | solution.py:111
  20.2 5.1 %copy-start.1 = (f32[64,128]{1,0:T(8,128)S(1)}, f32[64,128]{1,0:T(8,128)}, u32[]{:S(2)}) copy-start(f32[64,128]{1,0:T(8,128)} %param.6) | copy-start | bytes 98308
  31.7 13.2 %collective-permute-start.5 = (f32[64,128]{1,0:T(8,128)S(1)}, f32[64,128]{1,0:T(8,128)S(1)}, u32[]{:S(2)}, u32[]{:S(2)}) collective-permute-start(f32[64,128]{1,0:T(8,128)S(1)} %copy-done.1), channel_id=1, source_target_pairs={{6,0},{8,2},{10,4},{12,6},{14,8},{16,10},{18,12},{20,14},{22,16},{... | collective-permute-start | bytes 98312 | tf_op jit(solution)/shard_map/ppermute | solution.py:14
  37.1 13.8 %collective-permute-start.7 = (f32[64,128]{1,0:T(8,128)S(1)}, f32[64,128]{1,0:T(8,128)S(1)}, u32[]{:S(2)}, u32[]{:S(2)}) collective-permute-start(f32[64,128]{1,0:T(8,128)S(1)} %copy-done.1), channel_id=1, source_target_pairs={{8,0},{10,2},{12,4},{14,6},{16,8},{18,10},{20,12},{22,14},{24,16},... | collective-permute-start | bytes 98312 | tf_op jit(solution)/shard_map/ppermute | solution.py:14
  44.9 10.7 %collective-permute-start.3 = (f32[64,128]{1,0:T(8,128)S(1)}, f32[64,128]{1,0:T(8,128)S(1)}, u32[]{:S(2)}, u32[]{:S(2)}) collective-permute-start(f32[64,128]{1,0:T(8,128)S(1)} %copy-done.1), channel_id=1, source_target_pairs={{4,0},{6,2},{8,4},{10,6},{12,8},{14,10},{16,12},{18,14},{20,16},{2... | collective-permute-start | bytes 98312 | tf_op jit(solution)/shard_map/ppermute | solution.py:14
  50.9 34.3 %collective-permute-start.6 = (f32[64,256]{1,0:T(8,128)S(1)}, f32[64,256]{1,0:T(8,128)S(1)}, u32[]{:S(2)}, u32[]{:S(2)}) collective-permute-start(f32[64,256]{1,0:T(8,128)S(1)} %copy-done), channel_id=1, source_target_pairs={{8,0},{10,2},{12,4},{14,6},{16,8},{18,10},{20,12},{22,14},{24,16},... | collective-permute-start | bytes 196616 | tf_op jit(solution)/shard_map/ppermute | solution.py:14
  55.5 24.4 %collective-permute-start.8 = (f32[64,256]{1,0:T(8,128)S(1)}, f32[64,256]{1,0:T(8,128)S(1)}, u32[]{:S(2)}, u32[]{:S(2)}) collective-permute-start(f32[64,256]{1,0:T(8,128)S(1)} %copy-done), channel_id=1, source_target_pairs={{16,0},{18,2},{20,4},{22,6},{24,8},{26,10},{28,12},{30,14},{0,16},... | collective-permute-start | bytes 196616 | tf_op jit(solution)/shard_map/ppermute | solution.py:14
  93.9 0.7 copy-start.3
  94.6 196.6 %all-reduce.7.cloned.1.call-start = ((), (), s32[]{:S(2)}) async-start(), calls=%async_computation.3 | async-start | bytes 786432 | tf_op jit(solution)/shard_map/psum | solution.py:138
  147.7 1.1 copy-start.2
  149.1 3.6 copy-start.5
  150.2 9.2 %collective-permute-start.10 = (f32[64,128]{1,0:T(8,128)S(1)}, f32[64,128]{1,0:T(8,128)S(1)}, u32[]{:S(2)}, u32[]{:S(2)}) collective-permute-start(f32[64,128]{1,0:T(8,128)S(1)} %convolution_add_fusion.3), channel_id=1, source_target_pairs={{30,0},{0,2},{2,4},{4,6},{6,8},{8,10},{10,12},{12,14},{14,16},{16,... | collective-permute-start | bytes 98312 | tf_op jit(solution)/shard_map/ppermute | solution.py:14
  151.2 8.2 %collective-permute-start.11 = (f32[64,128]{1,0:T(8,128)S(1)}, f32[64,128]{1,0:T(8,128)S(1)}, u32[]{:S(2)}, u32[]{:S(2)}) collective-permute-start(f32[64,128]{1,0:T(8,128)S(1)} %convolution_add_fusion.2), channel_id=1, source_target_pairs={{28,0},{30,2},{0,4},{2,6},{4,8},{6,10},{8,12},{10,14},{12,16},{14,... | collective-permute-start | bytes 98312 | tf_op jit(solution)/shard_map/ppermute | solution.py:14
  152.9 6.5 %collective-permute-start.12 = (f32[64,128]{1,0:T(8,128)S(1)}, f32[64,128]{1,0:T(8,128)S(1)}, u32[]{:S(2)}, u32[]{:S(2)}) collective-permute-start(f32[64,128]{1,0:T(8,128)S(1)} %convolution_add_fusion.1), channel_id=1, source_target_pairs={{26,0},{28,2},{30,4},{0,6},{2,8},{4,10},{6,12},{8,14},{10,16},{12,... | collective-permute-start | bytes 98312 | tf_op jit(solution)/shard_map/ppermute | solution.py:14
  155.3 5.7 %collective-permute-start.13 = (f32[64,128]{1,0:T(8,128)S(1)}, f32[64,128]{1,0:T(8,128)S(1)}, u32[]{:S(2)}, u32[]{:S(2)}) collective-permute-start(f32[64,128]{1,0:T(8,128)S(1)} %get-tuple-element.26), channel_id=1, source_target_pairs={{24,0},{26,2},{28,4},{30,6},{0,8},{2,10},{4,12},{6,14},{8,16},{10,... | collective-permute-start | bytes 98312 | tf_op jit(solution)/shard_map/ppermute | solution.py:14
  155.9 5.2 %collective-permute-start.14 = (f32[64,128]{1,0:T(8,128)S(1)}, f32[64,128]{1,0:T(8,128)S(1)}, u32[]{:S(2)}, u32[]{:S(2)}) collective-permute-start(f32[64,128]{1,0:T(8,128)S(1)} %get-tuple-element.27), channel_id=1, source_target_pairs={{16,0},{18,2},{20,4},{22,6},{24,8},{26,10},{28,12},{30,14},{0,16},... | collective-permute-start | bytes 98312 | tf_op jit(solution)/shard_map/ppermute | solution.py:14
  161.3 193.7 %copy-start.4 = (f32[64,128]{1,0:T(8,128)}, f32[64,128]{1,0:T(8,128)S(1)}, u32[]{:S(2)}) copy-start(f32[64,128]{1,0:T(8,128)S(1)} %fusion.31) | copy-start | bytes 98308
  329.4 24.0 %copy-start.6 = (f32[256,128]{1,0:T(8,128)S(1)}, f32[256,128]{1,0:T(8,128)}, u32[]{:S(2)}) copy-start(f32[256,128]{1,0:T(8,128)} %get-tuple-element.22) | copy-start | bytes 393220
Sparse Core Ops, SparseCore 0:
  19.4 128.3 all-reduce.4
  162.5 128.7 all-reduce.6
Sparse Core Ops, SparseCore 1:
  94.7 10.7 reduce-scatter.1
where the time goes:
time: 364 us; the launch traced here: 363 us
  waiting for transfers between devices  183 us (50%)
  blocking collectives  57.9 us (16%)
  other arithmetic  56.6 us (16%)
  starting transfers between devices  23.3 us (6%)
  between operations  18.6 us (5%)
  matrix products  14.9 us (4%)
  local copies, waits for them, and re-layouts  8.57 us (2%)
    psum x1, waiting for transfers between devices, per_device(): gram_sum, projected = lax.psum((gram_part, projected_part), ('blk', 'row'))  129 us
    psum x1, waiting for transfers between devices, per_device(): pivot_feats = lax.psum(picked, ('blk', 'row'))  52.4 us
    another operation x6, other arithmetic, per_device(): factor = jnp.linalg.cholesky(gram)  34 us
    all_gather x6, blocking collectives, member_sweep(): arrived_feats = lax.all_gather(fetched[upper][0], 'row', axis=0, tiled=True)  30.5 us
    all_gather x6, blocking collectives, member_sweep(): lax.all_gather(fetched[upper][1], 'row', axis=0, tiled=True)  27.4 us
    ppermute x15, starting transfers between devices, shifted(): return lax.ppermute(block, axis, route)  23.2 us
    another operation x3, other arithmetic, per_device(): coefficients = jax.scipy.linalg.cho_solve((factor, True), projected)  19.7 us
  transfers between devices with their start and end apart: 18, of which 3 were waited for; matrix products, arithmetic and copies ran while one was open for 4% of the time, Pallas kernels for 0%

commit v1 on v0

--- a/solution.py
+++ b/solution.py
@@ -63,7 +63,13 @@
 def member_sweep(fetched, fetched_norms, upper, lower_group, block_rows):
     local_rows, probe_count = fetched[upper][1].shape
     column_sums = jnp.zeros((block_rows, probe_count), jnp.float32)
-    arrived_feats = lax.all_gather(fetched[upper][0], "row", axis=0, tiled=True)
+    arrived_feats = jnp.roll(
+        jnp.concatenate(
+            [fetched[upper][0], lax.ppermute(fetched[upper][0], "row", [(0, 1), (1, 0)])], axis=0
+        ),
+        lax.axis_index("row") * fetched[upper][0].shape[0],
+        axis=0,
+    )
     arrived_probes = lax.all_gather(fetched[upper][1], "row", axis=0, tiled=True)
     arrived_norms = jnp.sum(arrived_feats * arrived_feats, axis=1)
     updated = []

time: 364 us -> 382 us (1.049)
  waiting for transfers between devices: 183 us -> 227 us
  blocking collectives: 57.9 us -> 27.6 us
  starting transfers between devices: 23.3 us -> 28.3 us
    psum x1, waiting for transfers between devices: 52.4 us -> 83.2 us  [per_device(): pivot_feats = lax.psum(picked, ('blk', 'row'))]
    all_gather x6 -> x0, blocking collectives: 30.5 us -> none  [member_sweep(): arrived_feats = lax.all_gather(fetched[upper][0], 'row', axis=0, tiled=True)]
    reduce_scatter x1, waiting for transfers between devices: 0.03 us -> 11.4 us  [per_device(): lax.psum_scatter(jnp.stack(backward), 'row', scatter_dimension=1, tiled=T...]
    ppermute x0 -> x6, starting transfers between devices: none -> 6.27 us  [member_sweep(): lax.ppermute(fetched[upper][0], 'row', [(0, 1), (1, 0)])]
  transfers between devices with their start and end apart: 18 -> 24, of which waited for: 3 -> 5; matrix products, arithmetic and copies ran while one was open for 4% -> 3% of each run, Pallas kernels for 0% -> 0%
where the time goes in v1:
time: 382 us
  waiting for transfers between devices  227 us (59%)
  other arithmetic  57 us (15%)
  starting transfers between devices  28.3 us (7%)
  blocking collectives  27.6 us (7%)
  between operations  18.6 us (5%)
  matrix products  14.7 us (4%)
  local copies, waits for them, and re-layouts  8.88 us (2%)
    psum x1, waiting for transfers between devices, per_device(): gram_sum, projected = lax.psum((gram_part, projected_part), ('blk', 'row'))  129 us
    psum x1, waiting for transfers between devices, per_device(): pivot_feats = lax.psum(picked, ('blk', 'row'))  83.2 us
    another operation x6, other arithmetic, per_device(): factor = jnp.linalg.cholesky(gram)  34 us
    all_gather x6, blocking collectives, member_sweep(): lax.all_gather(fetched[upper][1], 'row', axis=0, tiled=True)  27.6 us
    ppermute x15, starting transfers between devices, shifted(): return lax.ppermute(block, axis, route)  21.9 us
    another operation x3, other arithmetic, per_device(): coefficients = jax.scipy.linalg.cho_solve((factor, True), projected)  19.7 us
    reduce_scatter x1, waiting for transfers between devices, per_device(): lax.psum_scatter(jnp.stack(backward), 'row', scatter_dimension=1, tiled=T...  11.4 us
  transfers between devices with their start and end apart: 24, of which 5 were waited for; matrix products, arithmetic and copies ran while one was open for 3% of the time, Pallas kernels for 0%

profile of v1, /device:TPU:0, one launch (start us, length us, event | category | flops | bytes accessed | tf_op | source)
XLA Modules:
  0.0 381.9 jit_solution(2442279915546600150)
XLA Ops:
  8.0 6.1 %collective-permute-start.4 = (f32[64,256]{1,0:T(8,128)}, f32[64,256]{1,0:T(8,128)S(1)}, u32[]{:S(2)}, u32[]{:S(2)}) collective-permute-start(f32[64,256]{1,0:T(8,128)} %param.7), channel_id=1, source_target_pairs={{4,0},{6,2},{8,4},{10,6},{12,8},{14,10},{16,12},{18,14},{20,16},{2... | collective-permute-start | bytes 196616 | tf_op jit(solution)/shard_map/ppermute | solution.py:14
  15.5 1.8 gather_fusion
  20.4 4.6 %all_gather.18 = f32[128,128]{1,0:T(8,128)S(1)} all-gather(f32[64,128]{1,0:T(8,128)S(1)} %copy-done.1), channel_id=1, replica_groups=mesh['blk'=16,'row'=2] {'row'}, dimensions={0}, use_global_device_ids=true | all-gather | bytes 98304 | tf_op jit(solution)/shard_map/all_gather | solution.py:73
  25.0 1.5 collective-permute-start
  26.5 4.6 %all_gather.23 = f32[128,128]{1,0:T(8,128)S(1)} all-gather(f32[64,128]{1,0:T(8,128)S(1)} %collective-permute-done.15), channel_id=1, replica_groups=mesh['blk'=16,'row'=2] {'row'}, dimensions={0}, use_global_device_ids=true | all-gather | bytes 98304 | tf_op jit(solution)/shard_map/all_gather | solution.py:73
  31.1 3.9 %collective-permute-start.12 = (f32[64,128]{1,0:T(8,128)S(1)}, f32[64,128]{1,0:T(8,128)S(1)}, u32[]{:S(2)}, u32[]{:S(2)}) collective-permute-start(f32[64,128]{1,0:T(8,128)S(1)} %copy-done.1), channel_id=1, source_target_pairs={{8,0},{10,2},{12,4},{14,6},{16,8},{18,10},{20,12},{22,14},{24,16},... | collective-permute-start | bytes 98312 | tf_op jit(solution)/shard_map/ppermute | solution.py:14
  35.0 4.6 %all_gather.19 = f32[128,128]{1,0:T(8,128)S(1)} all-gather(f32[64,128]{1,0:T(8,128)S(1)} %collective-permute-done.3), channel_id=1, replica_groups=mesh['blk'=16,'row'=2] {'row'}, dimensions={0}, use_global_device_ids=true | all-gather | bytes 98304 | tf_op jit(solution)/shard_map/all_gather | solution.py:73
  39.6 1.4 collective-permute-start.6
  41.0 4.6 %all_gather.21 = f32[128,128]{1,0:T(8,128)S(1)} all-gather(f32[64,128]{1,0:T(8,128)S(1)} %collective-permute-done.9), channel_id=1, replica_groups=mesh['blk'=16,'row'=2] {'row'}, dimensions={0}, use_global_device_ids=true | all-gather | bytes 98304 | tf_op jit(solution)/shard_map/all_gather | solution.py:73
  45.6 4.7 %all_gather.22 = f32[128,128]{1,0:T(8,128)S(1)} all-gather(f32[64,128]{1,0:T(8,128)S(1)} %collective-permute-done.12), channel_id=1, replica_groups=mesh['blk'=16,'row'=2] {'row'}, dimensions={0}, use_global_device_ids=true | all-gather | bytes 98304 | tf_op jit(solution)/shard_map/all_gather | solution.py:73
  50.3 4.6 %all_gather.20 = f32[128,128]{1,0:T(8,128)S(1)} all-gather(f32[64,128]{1,0:T(8,128)S(1)} %collective-permute-done.6), channel_id=1, replica_groups=mesh['blk'=16,'row'=2] {'row'}, dimensions={0}, use_global_device_ids=true | all-gather | bytes 98304 | tf_op jit(solution)/shard_map/all_gather | solution.py:73
  54.9 2.9 collective-permute-start.13
  59.1 1.6 collective-permute-start.2
  61.4 1.5 collective-permute-start.11
  63.6 83.2 %all-reduce.5.cloned.1.call-done = f32[256,256]{0,1:T(8,128)} async-done(((f32[256,256]{0,1:T(8,128)}), f32[256,256]{0,1:T(8,128)}) %all-reduce.5.cloned.1.call-update) | async-done | bytes 262160 | tf_op jit(solution)/shard_map/psum | solution.py:127
  146.8 1.1 multiply_reduce_fusion
  148.2 1.1 fusion.129
  156.0 11.4 %reduce-scatter.2.cloned.1.call-done = f32[6,64,128]{2,1,0:T(8,128)} async-done(((f32[6,128,128]{2,1,0:T(8,128)}), f32[6,64,128]{2,1,0:T(8,128)}) %reduce-scatter.2.cloned.1.call-update) | async-done | bytes 196624 | tf_op jit(solution)/shard_map/reduce_scatter | solution.py:117
  169.4 1.5 collective-permute-start.17
  171.2 2.4 collective-permute-start.18
  173.6 1.5 collective-permute-start.19
  175.1 1.4 collective-permute-start.20
  176.7 2.6 collective-permute-done.19
  181.2 128.7 %all-reduce.7.cloned.1.call-done = (f32[256,128]{1,0:T(8,128)}, f32[256,256]{0,1:T(8,128)}) async-done(((f32[256,128]{1,0:T(8,128)}, f32[256,256]{0,1:T(8,128)}), (f32[256,128]{1,0:T(8,128)}, f32[256,256]{0,1:T(8,128)})) %all-reduce.7.cloned.1.call-update) | async-done | bytes 393232 | tf_op jit(solution)/shard_map/psum | solution.py:144
  309.8 1.7 multiply_add_fusion
  311.7 11.7 %cholesky.49 = f32[128,128]{1,0:T(8,128)S(1)} custom-call(f32[128,128]{1,0:T(8,128)S(1)} %cholesky.115), custom_call_target="Cholesky" | custom-call | tf_op jit(solution)/shard_map/jit(cholesky)/cholesky | solution.py:147
  323.5 9.8 %custom-call.18 = f32[1,128,128]{1,2,0:T(8,128)S(1)} custom-call(f32[1,128,128]{2,1,0:T(8,128)S(1)} %get-tuple-element.42), custom_call_target="InvertDiagBlocksLowerTriangular" | custom-call | tf_op jit(solution)/shard_map/jit(cholesky)/cholesky | solution.py:147
  333.8 11.7 %cholesky.103 = f32[128,128]{1,0:T(8,128)S(1)} custom-call(f32[128,128]{1,0:T(8,128)S(1)} %convolution_subtract_fusion.2), custom_call_target="Cholesky" | custom-call | tf_op jit(solution)/shard_map/jit(cholesky)/cholesky | solution.py:147
  348.0 4.5 %while.1 = (s32[]{:T(128)}, f32[256,256]{0,1:T(8,128)S(1)}, s32[2,2]{1,0:T(2,128)S(1)}, f32[2,128,128]{2,1,0:T(8,128)S(1)}, s32[]{:T(128)}) while((s32[]{:T(128)}, f32[256,256]{0,1:T(8,128)S(1)}, s32[2,2]{1,0:T(2,128)S(1)}, f32[2,128,128]{2,1,0:T(8,128)S(1)}, s32[]{:T(128)}) %tuple.34), condition=%wide.while_cond, body=%wide.while_body.sunk | while | flops 2 | bytes 393321 | solution.py:148
  348.8 1.3 dynamic-slice.7
  351.0 1.3 dynamic-slice.7
  352.4 19.7 %custom-call.19 = f32[2,128,128]{1,2,0:T(8,128)S(1)} custom-call(f32[2,128,128]{2,1,0:T(8,128)S(1)} %get-tuple-element.10), custom_call_target="InvertDiagBlocksLowerTriangular" | custom-call | tf_op jit(solution)/shard_map/jit(_cho_solve)/triangular_solve | solution.py:148
  (129 shorter events, 22.6 us)
Async XLA Ops:
  8.0 138.8 %all-reduce.5.cloned.1.call-start = ((), (), s32[]{:S(2)}) async-start(), calls=%async_computation.2 | async-start | bytes 524288 | tf_op jit(solution)/shard_map/psum | solution.py:127
  8.0 50.4 %collective-permute-start.4 = (f32[64,256]{1,0:T(8,128)}, f32[64,256]{1,0:T(8,128)S(1)}, u32[]{:S(2)}, u32[]{:S(2)}) collective-permute-start(f32[64,256]{1,0:T(8,128)} %param.7), channel_id=1, source_target_pairs={{4,0},{6,2},{8,4},{10,6},{12,8},{14,10},{16,12},{18,14},{20,16},{2... | collective-permute-start | bytes 196616 | tf_op jit(solution)/shard_map/ppermute | solution.py:14
  14.1 45.0 %collective-permute-start.1 = (f32[64,256]{1,0:T(8,128)}, f32[64,256]{1,0:T(8,128)S(1)}, u32[]{:S(2)}, u32[]{:S(2)}) collective-permute-start(f32[64,256]{1,0:T(8,128)} %param.7), channel_id=1, source_target_pairs={{2,0},{4,2},{6,4},{8,6},{10,8},{12,10},{14,12},{16,14},{18,16},{20... | collective-permute-start | bytes 196616 | tf_op jit(solution)/shard_map/ppermute | solution.py:14
  14.1 17.0 %collective-permute-start.3 = (f32[64,128]{1,0:T(8,128)}, f32[64,128]{1,0:T(8,128)S(1)}, u32[]{:S(2)}, u32[]{:S(2)}) collective-permute-start(f32[64,128]{1,0:T(8,128)} %param.8), channel_id=1, source_target_pairs={{2,0},{4,2},{6,4},{8,6},{10,8},{12,10},{14,12},{16,14},{18,16},{20... | collective-permute-start | bytes 98312 | tf_op jit(solution)/shard_map/ppermute | solution.py:14
  14.8 24.8 %collective-permute-start.9 = (f32[64,128]{1,0:T(8,128)}, f32[64,128]{1,0:T(8,128)S(1)}, u32[]{:S(2)}, u32[]{:S(2)}) collective-permute-start(f32[64,128]{1,0:T(8,128)} %param.8), channel_id=1, source_target_pairs={{6,0},{8,2},{10,4},{12,6},{14,8},{16,10},{18,12},{20,14},{22,16},{... | collective-permute-start | bytes 98312 | tf_op jit(solution)/shard_map/ppermute | solution.py:14
  14.8 10.3 %collective-permute-start.15 = (f32[64,128]{1,0:T(8,128)}, f32[64,128]{1,0:T(8,128)S(1)}, u32[]{:S(2)}, u32[]{:S(2)}) collective-permute-start(f32[64,128]{1,0:T(8,128)} %param.8), channel_id=1, source_target_pairs={{16,0},{18,2},{20,4},{22,6},{24,8},{26,10},{28,12},{30,14},{0,16},... | collective-permute-start | bytes 98312 | tf_op jit(solution)/shard_map/ppermute | solution.py:14
  14.8 0.7 copy-start.7
  18.1 0.8 copy-start
  18.2 149.2 %reduce-scatter.2.cloned.1.call-start = ((), (), s32[]{:S(2)}) async-start(), calls=%async_computation.1 | async-start | bytes 589824 | tf_op jit(solution)/shard_map/reduce_scatter | solution.py:117
  19.1 1.3 copy-start.1
  25.0 29.9 %collective-permute-start = (f32[64,256]{1,0:T(8,128)S(1)}, f32[64,256]{1,0:T(8,128)S(1)}, u32[]{:S(2)}, u32[]{:S(2)}) collective-permute-start(f32[64,256]{1,0:T(8,128)S(1)} %copy-done), channel_id=1, source_target_pairs={{0,1},{1,0},{2,3},{3,2},{4,5},{5,4},{6,7},{7,6},{8,9},{9,8},{10,11... | collective-permute-start | bytes 196616 | tf_op jit(solution)/shard_map/ppermute | solution.py:68
  31.1 14.5 %collective-permute-start.12 = (f32[64,128]{1,0:T(8,128)S(1)}, f32[64,128]{1,0:T(8,128)S(1)}, u32[]{:S(2)}, u32[]{:S(2)}) collective-permute-start(f32[64,128]{1,0:T(8,128)S(1)} %copy-done.1), channel_id=1, source_target_pairs={{8,0},{10,2},{12,4},{14,6},{16,8},{18,10},{20,12},{22,14},{24,16},... | collective-permute-start | bytes 98312 | tf_op jit(solution)/shard_map/ppermute | solution.py:14
  39.6 10.7 %collective-permute-start.6 = (f32[64,128]{1,0:T(8,128)S(1)}, f32[64,128]{1,0:T(8,128)S(1)}, u32[]{:S(2)}, u32[]{:S(2)}) collective-permute-start(f32[64,128]{1,0:T(8,128)S(1)} %copy-done.1), channel_id=1, source_target_pairs={{4,0},{6,2},{8,4},{10,6},{12,8},{14,10},{16,12},{18,14},{20,16},{2... | collective-permute-start | bytes 98312 | tf_op jit(solution)/shard_map/ppermute | solution.py:14
  45.6 15.2 %collective-permute-start.7 = (f32[64,256]{1,0:T(8,128)S(1)}, f32[64,256]{1,0:T(8,128)S(1)}, u32[]{:S(2)}, u32[]{:S(2)}) collective-permute-start(f32[64,256]{1,0:T(8,128)S(1)} %copy-done), channel_id=1, source_target_pairs={{6,0},{8,2},{10,4},{12,6},{14,8},{16,10},{18,12},{20,14},{22,16},{... | collective-permute-start | bytes 196616 | tf_op jit(solution)/shard_map/ppermute | solution.py:14
  50.3 11.1 %collective-permute-start.10 = (f32[64,256]{1,0:T(8,128)S(1)}, f32[64,256]{1,0:T(8,128)S(1)}, u32[]{:S(2)}, u32[]{:S(2)}) collective-permute-start(f32[64,256]{1,0:T(8,128)S(1)} %copy-done), channel_id=1, source_target_pairs={{8,0},{10,2},{12,4},{14,6},{16,8},{18,10},{20,12},{22,14},{24,16},... | collective-permute-start | bytes 196616 | tf_op jit(solution)/shard_map/ppermute | solution.py:14
  54.9 8.1 %collective-permute-start.13 = (f32[64,256]{1,0:T(8,128)S(1)}, f32[64,256]{1,0:T(8,128)S(1)}, u32[]{:S(2)}, u32[]{:S(2)}) collective-permute-start(f32[64,256]{1,0:T(8,128)S(1)} %copy-done), channel_id=1, source_target_pairs={{16,0},{18,2},{20,4},{22,6},{24,8},{26,10},{28,12},{30,14},{0,16},... | collective-permute-start | bytes 196616 | tf_op jit(solution)/shard_map/ppermute | solution.py:14
  58.4 90.9 %collective-permute-start.5 = (f32[64,256]{1,0:T(8,128)S(1)}, f32[64,256]{1,0:T(8,128)S(1)}, u32[]{:S(2)}, u32[]{:S(2)}) collective-permute-start(f32[64,256]{1,0:T(8,128)S(1)} %collective-permute-done.4), channel_id=1, source_target_pairs={{0,1},{1,0},{2,3},{3,2},{4,5},{5,4},{6,7},{7,6},{8,9},{9,8},{10,11... | collective-permute-start | bytes 196616 | tf_op jit(solution)/shard_map/ppermute | solution.py:68
  59.1 90.6 %collective-permute-start.2 = (f32[64,256]{1,0:T(8,128)S(1)}, f32[64,256]{1,0:T(8,128)S(1)}, u32[]{:S(2)}, u32[]{:S(2)}) collective-permute-start(f32[64,256]{1,0:T(8,128)S(1)} %collective-permute-done.1), channel_id=1, source_target_pairs={{0,1},{1,0},{2,3},{3,2},{4,5},{5,4},{6,7},{7,6},{8,9},{9,8},{10,11... | collective-permute-start | bytes 196616 | tf_op jit(solution)/shard_map/ppermute | solution.py:68
  60.8 90.0 %collective-permute-start.8 = (f32[64,256]{1,0:T(8,128)S(1)}, f32[64,256]{1,0:T(8,128)S(1)}, u32[]{:S(2)}, u32[]{:S(2)}) collective-permute-start(f32[64,256]{1,0:T(8,128)S(1)} %collective-permute-done.7), channel_id=1, source_target_pairs={{0,1},{1,0},{2,3},{3,2},{4,5},{5,4},{6,7},{7,6},{8,9},{9,8},{10,11... | collective-permute-start | bytes 196616 | tf_op jit(solution)/shard_map/ppermute | solution.py:68
  61.4 90.2 %collective-permute-start.11 = (f32[64,256]{1,0:T(8,128)S(1)}, f32[64,256]{1,0:T(8,128)S(1)}, u32[]{:S(2)}, u32[]{:S(2)}) collective-permute-start(f32[64,256]{1,0:T(8,128)S(1)} %collective-permute-done.10), channel_id=1, source_target_pairs={{0,1},{1,0},{2,3},{3,2},{4,5},{5,4},{6,7},{7,6},{8,9},{9,8},{10,11... | collective-permute-start | bytes 196616 | tf_op jit(solution)/shard_map/ppermute | solution.py:68
  62.9 89.5 %collective-permute-start.14 = (f32[64,256]{1,0:T(8,128)S(1)}, f32[64,256]{1,0:T(8,128)S(1)}, u32[]{:S(2)}, u32[]{:S(2)}) collective-permute-start(f32[64,256]{1,0:T(8,128)S(1)} %collective-permute-done.13), channel_id=1, source_target_pairs={{0,1},{1,0},{2,3},{3,2},{4,5},{5,4},{6,7},{7,6},{8,9},{9,8},{10,11... | collective-permute-start | bytes 196616 | tf_op jit(solution)/shard_map/ppermute | solution.py:68
  146.8 1.1 copy-start.2
  154.3 0.7 copy-start.3
  155.1 154.7 %all-reduce.7.cloned.1.call-start = ((), (), s32[]{:S(2)}) async-start(), calls=%async_computation.3 | async-start | bytes 786432 | tf_op jit(solution)/shard_map/psum | solution.py:144
  167.4 3.6 copy-start.5
  168.4 8.3 %collective-permute-start.16 = (f32[64,128]{1,0:T(8,128)S(1)}, f32[64,128]{1,0:T(8,128)S(1)}, u32[]{:S(2)}, u32[]{:S(2)}) collective-permute-start(f32[64,128]{1,0:T(8,128)S(1)} %convolution_add_fusion.3), channel_id=1, source_target_pairs={{30,0},{0,2},{2,4},{4,6},{6,8},{8,10},{10,12},{12,14},{14,16},{16,... | collective-permute-start | bytes 98312 | tf_op jit(solution)/shard_map/ppermute | solution.py:14
  169.4 7.3 %collective-permute-start.17 = (f32[64,128]{1,0:T(8,128)S(1)}, f32[64,128]{1,0:T(8,128)S(1)}, u32[]{:S(2)}, u32[]{:S(2)}) collective-permute-start(f32[64,128]{1,0:T(8,128)S(1)} %convolution_add_fusion.2), channel_id=1, source_target_pairs={{28,0},{30,2},{0,4},{2,6},{4,8},{6,10},{8,12},{10,14},{12,16},{14,... | collective-permute-start | bytes 98312 | tf_op jit(solution)/shard_map/ppermute | solution.py:14
  171.2 5.5 %collective-permute-start.18 = (f32[64,128]{1,0:T(8,128)S(1)}, f32[64,128]{1,0:T(8,128)S(1)}, u32[]{:S(2)}, u32[]{:S(2)}) collective-permute-start(f32[64,128]{1,0:T(8,128)S(1)} %convolution_add_fusion.1), channel_id=1, source_target_pairs={{26,0},{28,2},{30,4},{0,6},{2,8},{4,10},{6,12},{8,14},{10,16},{12,... | collective-permute-start | bytes 98312 | tf_op jit(solution)/shard_map/ppermute | solution.py:14
  173.6 5.7 %collective-permute-start.19 = (f32[64,128]{1,0:T(8,128)S(1)}, f32[64,128]{1,0:T(8,128)S(1)}, u32[]{:S(2)}, u32[]{:S(2)}) collective-permute-start(f32[64,128]{1,0:T(8,128)S(1)} %get-tuple-element.39), channel_id=1, source_target_pairs={{24,0},{26,2},{28,4},{30,6},{0,8},{2,10},{4,12},{6,14},{8,16},{10,... | collective-permute-start | bytes 98312 | tf_op jit(solution)/shard_map/ppermute | solution.py:14
  175.1 4.8 %collective-permute-start.20 = (f32[64,128]{1,0:T(8,128)S(1)}, f32[64,128]{1,0:T(8,128)S(1)}, u32[]{:S(2)}, u32[]{:S(2)}) collective-permute-start(f32[64,128]{1,0:T(8,128)S(1)} %get-tuple-element.40), channel_id=1, source_target_pairs={{16,0},{18,2},{20,4},{22,6},{24,8},{26,10},{28,12},{30,14},{0,16},... | collective-permute-start | bytes 98312 | tf_op jit(solution)/shard_map/ppermute | solution.py:14
  180.1 193.6 %copy-start.4 = (f32[64,128]{1,0:T(8,128)}, f32[64,128]{1,0:T(8,128)S(1)}, u32[]{:S(2)}) copy-start(f32[64,128]{1,0:T(8,128)S(1)} %fusion.60) | copy-start | bytes 98308
  348.0 24.2 %copy-start.6 = (f32[256,128]{1,0:T(8,128)S(1)}, f32[256,128]{1,0:T(8,128)}, u32[]{:S(2)}) copy-start(f32[256,128]{1,0:T(8,128)} %get-tuple-element.23) | copy-start | bytes 393220
Sparse Core Ops, SparseCore 0:
  18.3 128.4 all-reduce.4
  181.3 128.5 all-reduce.6
Sparse Core Ops, SparseCore 1:
  155.2 12.2 reduce-scatter.1
